TPU v7x, 32 devices: a whole 2x2x4 slice. The times are simulated.
32 devices in a mesh: rows: 8 (over z, y), cols: 4 (over x, core).
Axes of the slice: x: 2, y: 2, z: 4, core: 2. Of those that a mesh axis runs over, the one named last changes fastest.
Arguments:
- adjacency_tiles: bfloat16 [192, 12, 128, 128], P(('rows', 'cols')), may hold values from 2.170139e-08 to 0.25
- col_block: int32 [192, 12], P(('rows', 'cols')), may hold values from 0 to 191, as said below
- label_prior: float32 [24576, 256], P(('rows', 'cols')), may hold values from 0.05 to 20.1
- seed_label: int32 [24576], P(('rows', 'cols')), may hold values from 0 to 255
- seed_mask: int32 [24576], P(('rows', 'cols')), may hold values 0 or 1
Outputs:
- labels: float32 [24576, 256], P(('rows', 'cols'))
Inputs may be any that keep to these rules, and one draw needn't show every extreme that they name: Row block b is held by device b // 6 of rows+cols, whose rows group is b // (6 * 4). col_block[b, 0] = b. For each device, all its tiles that reference blocks of another rows group reference one and the same block of that group, and each device references every rows group.
All inputs are finite; a program needn't handle non-finite values. No bound on the sum of `seed_mask` on one device may be relied on, other than what follows from the above.
Results may differ from a plain program's by a relative error of at most 0.00041.
Values may be sent and summed in bfloat16 or wider, within the bound.
A program may use at most 64 MiB of HBM per device.

v0:
```python
import functools

import jax
import jax.numpy as jnp
from jax import lax
from jax.experimental import pallas as pl
from jax.experimental.pallas import tpu as pltpu
from jax.sharding import PartitionSpec as P

HOPS = 4
CHUNK_PARTS = (1, 1, 2, 2, 2)
CHUNKS = len(CHUNK_PARTS)
ALPHA = 0.85
SEED_BOOST = 8.0
LANES = 128
VMEM_LIMIT = 67_043_328
SPARE = 64 * 1024
MESH = pl.DeviceIdType.MESH


def kernel(
    n_rows, n_cols, blocks_dev, degree, block_rows, classes,
    col_block_hbm, prior_hbm, label_hbm, mask_hbm, adj_hbm, out_ref,
    tables, remote, reply, adj, anchor_ref, index_ref, wanted_ref, asked_v, asked_s,
    col_block_ref, prior_ref, label_ref, mask_ref, in_sem,
    adj_sem, asked_send, asked_recv, asked_copy,
    near_send, near_recv, far_send, far_recv, fwd_send, fwd_recv, rep_send, rep_recv,
):
    row = lax.axis_index("rows")
    col = lax.axis_index("cols")
    group = n_cols * blocks_dev
    width = 2 if n_cols % 2 == 0 else 1
    pairs = n_cols // width
    pair, low = col // width, col % width
    mate = pair * width + (width - 1 - low)
    unit = block_rows // sum(CHUNK_PARTS)
    starts = [unit * sum(CHUNK_PARTS[:q]) for q in range(CHUNKS)]
    sizes = [unit * part for part in CHUNK_PARTS]
    peers = n_rows - 1

    def far_col(j):
        return ((pair + j) % pairs) * width + low

    def from_col(j):
        return ((pair + pairs - j) % pairs) * width + low

    def each_peer(body):
        half = n_rows // 2
        def step(i):
            if isinstance(i, int):
                d = half + ((i + 1) // 2) * (1 - 2 * (i % 2))
            else:
                d = half + lax.div(i + 1, 2) * (1 - 2 * lax.rem(i, 2))
            body((row + d + n_rows) % n_rows)
        if n_rows <= 8:
            for i in range(peers):
                step(i)
        else:
            def loop(i, carry):
                step(i)
                return carry
            lax.fori_loop(0, peers, loop, 0)

    adj_copy = pltpu.make_async_copy(adj_hbm, adj, adj_sem)
    loads = [
        pltpu.make_async_copy(source, target, in_sem.at[i])
        for i, (source, target) in enumerate([
            (label_hbm, label_ref),
            (mask_hbm, mask_ref),
            (prior_hbm, prior_ref),
            (col_block_hbm, col_block_ref),
        ])
    ]
    for load in loads:
        load.start()
    adj_copy.start()

    barrier = pltpu.get_barrier_semaphore()
    greeted = peers
    if width == 2:
        pl.semaphore_signal(barrier, inc=1, device_id=(row, mate), device_id_type=MESH)
        greeted += 1
    for j in range(1, pairs):
        pl.semaphore_signal(barrier, inc=1, device_id=(row, far_col(j)), device_id_type=MESH)
        greeted += 1
    each_peer(
        lambda other: pl.semaphore_signal(
            barrier, inc=1, device_id=(other, col), device_id_type=MESH
        )
    )
    def keep(p, b, labels):
        sent = labels.astype(jnp.bfloat16)
        for q in range(CHUNKS):
            tables[p][q][col * blocks_dev + b] = sent[starts[q] : starts[q] + sizes[q], :]

    for load in loads:
        load.wait()
    code = jnp.where(mask_ref[...] > 0, label_ref[...], -1)
    for b in range(blocks_dev):
        here = slice(b * block_rows, (b + 1) * block_rows)
        across = jnp.broadcast_to(code[b : b + 1, :], (block_rows, block_rows)).T
        class_id = lax.broadcasted_iota(jnp.int32, (block_rows, classes), 1)
        across = jnp.concatenate([across] * (classes // block_rows), axis=1)
        raw = prior_ref[here, :] + jnp.where(class_id == across, SEED_BOOST, 0.0)
        anchor = raw * (classes / jnp.sum(raw, axis=1, keepdims=True))
        anchor_ref[here, :] = anchor
        keep(0, b, anchor)
    pl.semaphore_wait(barrier, greeted)

    def part(p, owner, q):
        return tables[p][q].at[pl.ds(owner * blocks_dev, blocks_dev)]

    def near(p, q):
        ref = part(p, col, q)
        return pltpu.make_async_remote_copy(
            src_ref=ref, dst_ref=ref, send_sem=near_send.at[p, q], recv_sem=near_recv.at[p, q],
            device_id=(row, mate), device_id_type=MESH,
        )

    def far(p, j, q):
        ref = part(p, col, q)
        return pltpu.make_async_remote_copy(
            src_ref=ref, dst_ref=ref,
            send_sem=far_send.at[p, j - 1, q], recv_sem=far_recv.at[p, j - 1, q],
            device_id=(row, far_col(j)), device_id_type=MESH,
        )

    def forward(p, j, q):
        ref = part(p, from_col(j), q)
        return pltpu.make_async_remote_copy(
            src_ref=ref, dst_ref=ref,
            send_sem=fwd_send.at[p, j - 1, q], recv_sem=fwd_recv.at[p, j - 1, q],
            device_id=(row, mate), device_id_type=MESH,
        )

    def start_gather(p):
        for q in range(CHUNKS):
            for j in range(1, pairs):
                far(p, j, q).start()
            if width == 2:
                near(p, q).start()

    start_gather(0)

    lane = lax.broadcasted_iota(jnp.int32, wanted_ref.shape, 1)
    wanted = jnp.zeros(wanted_ref.shape, jnp.int32)
    for b in range(blocks_dev):
        for k in range(degree):
            block = col_block_ref[b, k]
            owner = lax.div(block, group)
            within = block - owner * group
            index_ref[b * degree + k] = jnp.where(owner == row, within, group + owner)
            wanted = jnp.where(lane == owner, within, wanted)
    wanted_ref[...] = wanted

    def send_wanted(other):
        pltpu.make_async_remote_copy(
            src_ref=wanted_ref, dst_ref=asked_v.at[row], send_sem=asked_send, recv_sem=asked_recv,
            device_id=(other, col), device_id_type=MESH,
        ).start()

    each_peer(send_wanted)
    all_asked = asked_v.at[pl.ds(0, peers)]
    pltpu.make_async_copy(all_asked, all_asked, asked_recv).wait()
    pltpu.make_async_copy(all_asked, all_asked, asked_send).wait()
    to_scalar = pltpu.make_async_copy(asked_v, asked_s, asked_copy)
    to_scalar.start()
    to_scalar.wait()
    adj_copy.wait()

    def operand(p, b, k):
        index = index_ref[b * degree + k]
        return [tables[p][q][index] for q in range(CHUNKS)]

    def hop(p, last):
        for q in range(CHUNKS):
            rows_q = pl.ds(starts[q], sizes[q])
            for j in range(1, pairs):
                far(p, j, q).wait_recv()
                if width == 2:
                    forward(p, j, q).start()
            if width == 2:
                near(p, q).wait_recv()
                for j in range(1, pairs):
                    forward(p, j, q).wait_recv()

            def answer(other):
                reply[other, rows_q, :] = tables[p][q][asked_s[other, 0, row]]
                pltpu.make_async_remote_copy(
                    src_ref=reply.at[other, rows_q, :],
                    dst_ref=remote.at[p, row, rows_q, :],
                    send_sem=rep_send.at[p], recv_sem=rep_recv.at[p],
                    device_id=(other, col), device_id_type=MESH,
                ).start()

            each_peer(answer)
        got = remote.at[p, pl.ds(0, peers)]
        pltpu.make_async_copy(got, got, rep_recv.at[p]).wait()

        def fold(other):
            for q in range(CHUNKS):
                tables[p][q][group + other] = remote[p, other, pl.ds(starts[q], sizes[q]), :]

        each_peer(fold)

        step = 2 if degree % 2 == 0 else 1
        for b in range(blocks_dev):
            spread = jnp.zeros((block_rows, classes), jnp.float32)
            for k in range(0, degree, step):
                lhs = jnp.concatenate([adj[b, k + i] for i in range(step)], axis=1)
                rhs = jnp.concatenate(sum([operand(p, b, k + i) for i in range(step)], []), axis=0)
                spread = spread + jnp.dot(lhs, rhs, preferred_element_type=jnp.float32)
            here = slice(b * block_rows, (b + 1) * block_rows)
            blended = ALPHA * spread + (1.0 - ALPHA) * anchor_ref[here, :]
            labels = blended * (classes / jnp.sum(blended, axis=1, keepdims=True))
            out_ref[here, :] = labels
            keep(1 - p, b, labels)

        for q in range(CHUNKS):
            for j in range(1, pairs):
                far(p, j, q).wait_send()
                if width == 2:
                    forward(p, j, q).wait_send()
            if width == 2:
                near(p, q).wait_send()
        sent = reply.at[pl.ds(0, peers)]
        pltpu.make_async_copy(sent, sent, rep_send.at[p]).wait()

        if not last:
            start_gather(1 - p)

    for h in range(HOPS):
        hop(h % 2, h == HOPS - 1)


def local(adjacency_tiles, col_block, label_prior, seed_label, seed_mask):
    blocks_dev, degree, block_rows, _ = adjacency_tiles.shape
    nodes, classes = label_prior.shape
    n_rows = lax.axis_size("rows")
    n_cols = lax.axis_size("cols")
    group = n_cols * blocks_dev
    padded = -(-n_rows // LANES) * LANES
    pairs = max(n_cols // 2 if n_cols % 2 == 0 else n_cols, 2)
    unit = block_rows // sum(CHUNK_PARTS)
    dma = pltpu.SemaphoreType.DMA
    vmem = pl.BlockSpec(memory_space=pltpu.VMEM)
    return pl.pallas_call(
        functools.partial(kernel, n_rows, n_cols, blocks_dev, degree, block_rows, classes),
        out_shape=jax.ShapeDtypeStruct((nodes, classes), jnp.float32),
        in_specs=[
            pl.BlockSpec(memory_space=pl.ANY),
        ] * 5,
        out_specs=vmem,
        scratch_shapes=[
            [
                [
                    pltpu.VMEM((group + n_rows, unit * part, classes), jnp.bfloat16)
                    for part in CHUNK_PARTS
                ]
                for _ in range(2)
            ],
            pltpu.VMEM((2, n_rows, block_rows, classes), jnp.bfloat16),
            pltpu.VMEM((n_rows, block_rows, classes), jnp.bfloat16),
            pltpu.VMEM(adjacency_tiles.shape, jnp.bfloat16),
            pltpu.VMEM((nodes, classes), jnp.float32),
            pltpu.SMEM((blocks_dev * degree,), jnp.int32),
            pltpu.VMEM((1, padded), jnp.int32),
            pltpu.VMEM((n_rows, 1, padded), jnp.int32),
            pltpu.SMEM((n_rows, 1, padded), jnp.int32),
            pltpu.SMEM(col_block.shape, jnp.int32),
            pltpu.VMEM((nodes, classes), jnp.float32),
            pltpu.VMEM((blocks_dev, block_rows), jnp.int32),
            pltpu.VMEM((blocks_dev, block_rows), jnp.int32),
            dma((4,)),
            dma, dma, dma, dma,
            dma((2, CHUNKS)), dma((2, CHUNKS)),
            dma((2, pairs - 1, CHUNKS)), dma((2, pairs - 1, CHUNKS)),
            dma((2, pairs - 1, CHUNKS)), dma((2, pairs - 1, CHUNKS)),
            dma((2,)), dma((2,)),
        ],
        compiler_params=pltpu.CompilerParams(
            collective_id=0, has_side_effects=True, vmem_limit_bytes=VMEM_LIMIT - 4 * nodes * classes - SPARE
        ),
    )(
        col_block,
        label_prior,
        seed_label.reshape(blocks_dev, block_rows),
        seed_mask.reshape(blocks_dev, block_rows),
        adjacency_tiles,
    )


def solution(mesh):
    in_specs = (
        P(("rows", "cols"), None, None, None),
        P(("rows", "cols"), None),
        P(("rows", "cols"), None),
        P(("rows", "cols")),
        P(("rows", "cols")),
    )
    out_specs = P(("rows", "cols"), None)
    return jax.shard_map(local, mesh=mesh, in_specs=in_specs, out_specs=out_specs, check_vma=False)
```

profile of v0, /device:TPU:0, one launch (start us, length us, event | category | flops | bytes accessed | tf_op | source)
XLA Modules:
  0.0 85.5 jit_solution(5028140279065129013)
XLA Ops:
  0.0 83.4 %shard_map.55 = f32[768,256]{1,0:T(8,128)} custom-call(s32[6,12]{1,0:T(8,128)} %col_block_hbm.1, f32[768,256]{1,0:T(8,128)} %prior_hbm.1, s32[6,128]{1,0:T(8,128)} %bitcast.2, s32[6,128]{1,0:T(8,128)} %bitcast.3, bf16[6,12,128,128]{3,2,1,0:T(8,128)(2,1)} %adj_hbm.1), custom_call_target="tpu_custom_call" | custom-call | tf_op jit(solution)/shard_map/pallas_call | solution.py:247
  83.4 2.1 %copy.7 = f32[768,256]{1,0:T(8,128)} copy(f32[768,256]{1,0:T(8,128)} %shard_map.55) | data formatting | bytes 1572864
where the time goes:
time: 85.7 us; the launch traced here: 85.5 us
  Pallas kernels  83.4 us (97%)
  local copies, waits for them, and re-layouts  2.06 us (2%)
    pallas_call x1, Pallas kernels, local(): pl.pallas_call(functools.partial(kernel, n_rows, n_cols, blocks_dev, degr...  83.4 us
    unnamed x1, local copies, waits for them, and re-layouts  2.06 us

commit v1 on v0

v1 whole, which is shorter than its diff:
```python
import functools

import jax
import jax.numpy as jnp
from jax import lax
from jax.experimental import pallas as pl
from jax.experimental.pallas import tpu as pltpu
from jax.sharding import PartitionSpec as P

HOPS = 4
STREAMS = 2
CHUNK_PARTS = (1, 1, 2, 4)
CHUNKS = len(CHUNK_PARTS)
ALPHA = 0.85
SEED_BOOST = 8.0
LANES = 128
VMEM_LIMIT = 67_043_328
SPARE = 64 * 1024
MESH = pl.DeviceIdType.MESH


def kernel(
    n_rows, n_cols, blocks_dev, degree, block_rows, classes,
    col_block_hbm, prior_hbm, label_hbm, mask_hbm, adj_hbm, out_ref,
    tables, remote, reply, sums, sums_remote, sums_reply, sums_part, scale_ref,
    adj, anchor_ref, index_ref, wanted_ref, asked_v, asked_s,
    col_block_ref, prior_ref, label_ref, mask_ref, in_sem,
    adj_sem, asked_send, asked_recv, asked_copy,
    near_send, near_recv, far_send, far_recv, fwd_send, fwd_recv, rep_send, rep_recv,
    sums_send, sums_recv, srep_send, srep_recv,
):
    row = lax.axis_index("rows")
    col = lax.axis_index("cols")
    group = n_cols * blocks_dev
    lanes = classes // STREAMS
    width = 2 if n_cols % 2 == 0 else 1
    pairs = n_cols // width
    pair, low = col // width, col % width
    mate = pair * width + (width - 1 - low)
    unit = block_rows // sum(CHUNK_PARTS)
    starts = [unit * sum(CHUNK_PARTS[:q]) for q in range(CHUNKS)]
    sizes = [unit * part for part in CHUNK_PARTS]
    peers = n_rows - 1

    def far_col(j):
        return ((pair + j) % pairs) * width + low

    def from_col(j):
        return ((pair + pairs - j) % pairs) * width + low

    def each_peer(body):
        half = n_rows // 2
        def step(i):
            if isinstance(i, int):
                d = half + ((i + 1) // 2) * (1 - 2 * (i % 2))
            else:
                d = half + lax.div(i + 1, 2) * (1 - 2 * lax.rem(i, 2))
            body((row + d + n_rows) % n_rows)
        if n_rows <= 8:
            for i in range(peers):
                step(i)
        else:
            def loop(i, carry):
                step(i)
                return carry
            lax.fori_loop(0, peers, loop, 0)

    adj_copy = pltpu.make_async_copy(adj_hbm, adj, adj_sem)
    loads = [
        pltpu.make_async_copy(source, target, in_sem.at[i])
        for i, (source, target) in enumerate([
            (label_hbm, label_ref),
            (mask_hbm, mask_ref),
            (prior_hbm, prior_ref),
            (col_block_hbm, col_block_ref),
        ])
    ]
    for load in loads:
        load.start()
    adj_copy.start()

    barrier = pltpu.get_barrier_semaphore()
    for j in range(1, n_cols):
        pl.semaphore_signal(
            barrier, inc=1, device_id=(row, (col + j) % n_cols), device_id_type=MESH
        )
    each_peer(
        lambda other: pl.semaphore_signal(
            barrier, inc=1, device_id=(other, col), device_id_type=MESH
        )
    )

    ones = jnp.ones((8, lanes), jnp.bfloat16)

    def keep(p, s, b, labels):
        sent = labels.astype(jnp.bfloat16)
        for q in range(CHUNKS):
            tables[p][s][q][col * blocks_dev + b] = sent[starts[q] : starts[q] + sizes[q], :]
        total = lax.dot_general(
            ones, sent, (((1,), (1,)), ((), ())), preferred_element_type=jnp.float32
        )[:1, :]
        if s > 0:
            total = total + sums_part[b]
        if s < STREAMS - 1:
            sums_part[b] = total
        else:
            sums[p][col * blocks_dev + b] = total

    for load in loads:
        load.wait()
    code = jnp.where(mask_ref[...] > 0, label_ref[...], -1)
    for b in range(blocks_dev):
        here = slice(b * block_rows, (b + 1) * block_rows)
        across = jnp.broadcast_to(code[b : b + 1, :], (block_rows, block_rows)).T
        class_id = lax.broadcasted_iota(jnp.int32, (block_rows, classes), 1)
        across = jnp.concatenate([across] * (classes // block_rows), axis=1)
        raw = prior_ref[here, :] + jnp.where(class_id == across, SEED_BOOST, 0.0)
        anchor = raw * (classes / jnp.sum(raw, axis=1, keepdims=True))
        anchor_ref[here, :] = anchor
        for s in range(STREAMS):
            keep(0, s, b, anchor[:, s * lanes : (s + 1) * lanes])

    lane = lax.broadcasted_iota(jnp.int32, wanted_ref.shape, 1)
    wanted = jnp.zeros(wanted_ref.shape, jnp.int32)
    for b in range(blocks_dev):
        for k in range(degree):
            block = col_block_ref[b, k]
            owner = lax.div(block, group)
            within = block - owner * group
            index_ref[b * degree + k] = jnp.where(owner == row, within, group + owner)
            wanted = jnp.where(lane == owner, within, wanted)
    wanted_ref[...] = wanted

    pl.semaphore_wait(barrier, n_cols - 1 + peers)

    def send_wanted(other):
        pltpu.make_async_remote_copy(
            src_ref=wanted_ref, dst_ref=asked_v.at[row], send_sem=asked_send, recv_sem=asked_recv,
            device_id=(other, col), device_id_type=MESH,
        ).start()

    each_peer(send_wanted)

    def part(p, s, owner, q):
        return tables[p][s][q].at[pl.ds(owner * blocks_dev, blocks_dev)]

    def near(p, s, q):
        ref = part(p, s, col, q)
        return pltpu.make_async_remote_copy(
            src_ref=ref, dst_ref=ref,
            send_sem=near_send.at[p, s, q], recv_sem=near_recv.at[p, s, q],
            device_id=(row, mate), device_id_type=MESH,
        )

    def far(p, s, j, q):
        ref = part(p, s, col, q)
        return pltpu.make_async_remote_copy(
            src_ref=ref, dst_ref=ref,
            send_sem=far_send.at[p, s, j - 1, q], recv_sem=far_recv.at[p, s, j - 1, q],
            device_id=(row, far_col(j)), device_id_type=MESH,
        )

    def forward(p, s, j, q):
        ref = part(p, s, from_col(j), q)
        return pltpu.make_async_remote_copy(
            src_ref=ref, dst_ref=ref,
            send_sem=fwd_send.at[p, s, j - 1, q], recv_sem=fwd_recv.at[p, s, j - 1, q],
            device_id=(row, mate), device_id_type=MESH,
        )

    def sums_to(p, j):
        ref = sums[p].at[pl.ds(col * blocks_dev, blocks_dev)]
        return pltpu.make_async_remote_copy(
            src_ref=ref, dst_ref=ref,
            send_sem=sums_send.at[p, j - 1], recv_sem=sums_recv.at[p, j - 1],
            device_id=(row, (col + j) % n_cols), device_id_type=MESH,
        )

    def start_sums(p):
        for j in range(1, n_cols):
            sums_to(p, j).start()

    def start_gather(p, s):
        for q in range(CHUNKS):
            for j in range(1, pairs):
                far(p, s, j, q).start()
            if width == 2:
                near(p, s, q).start()

    def relay_sums(p):
        for j in range(1, n_cols):
            sums_to(p, j).wait_recv()

        def answer(other):
            sums_reply[other] = sums[p][asked_s[other, 0, row]]
            pltpu.make_async_remote_copy(
                src_ref=sums_reply.at[other], dst_ref=sums_remote.at[p, row],
                send_sem=srep_send.at[p], recv_sem=srep_recv.at[p],
                device_id=(other, col), device_id_type=MESH,
            ).start()

        each_peer(answer)

    def relay(p, s):
        for q in range(CHUNKS):
            rows_q = pl.ds(starts[q], sizes[q])
            for j in range(1, pairs):
                far(p, s, j, q).wait_recv()
                if width == 2:
                    forward(p, s, j, q).start()
            if width == 2:
                near(p, s, q).wait_recv()
                for j in range(1, pairs):
                    forward(p, s, j, q).wait_recv()

            def answer(other):
                reply[s, other, rows_q, :] = tables[p][s][q][asked_s[other, 0, row]]
                pltpu.make_async_remote_copy(
                    src_ref=reply.at[s, other, rows_q, :],
                    dst_ref=remote.at[p, s, row, rows_q, :],
                    send_sem=rep_send.at[p, s], recv_sem=rep_recv.at[p, s],
                    device_id=(other, col), device_id_type=MESH,
                ).start()

            each_peer(answer)

    def operand(p, s, b, k):
        index = index_ref[b * degree + k]
        return [tables[p][s][q][index] for q in range(CHUNKS)]

    def row_scale(p, b):
        here = slice(b * block_rows, (b + 1) * block_rows)
        total = jnp.zeros((block_rows, block_rows), jnp.float32)
        for k in range(degree):
            total = total + adj[b, k].astype(jnp.float32) * sums[p][index_ref[b * degree + k]]
        rest = anchor_ref[here, :block_rows]
        for i in range(1, classes // block_rows):
            rest = rest + anchor_ref[here, i * block_rows : (i + 1) * block_rows]
        total = ALPHA * total + (1.0 - ALPHA) * rest
        return classes / jnp.sum(total, axis=1, keepdims=True)

    def finish(h, s):
        p, last = h % 2, h == HOPS - 1
        got = remote.at[p, s, pl.ds(0, peers)]
        pltpu.make_async_copy(got, got, rep_recv.at[p, s]).wait()
        if s == 0:
            got = sums_remote.at[p, pl.ds(0, peers)]
            pltpu.make_async_copy(got, got, srep_recv.at[p]).wait()

        def fold(other):
            for q in range(CHUNKS):
                tables[p][s][q][group + other] = remote[p, s, other, pl.ds(starts[q], sizes[q]), :]
            if s == 0:
                sums[p][group + other] = sums_remote[p, other]

        each_peer(fold)

        step = 2 if degree % 2 == 0 else 1
        mine = slice(s * lanes, (s + 1) * lanes)
        for b in range(blocks_dev):
            here = slice(b * block_rows, (b + 1) * block_rows)
            spread = jnp.zeros((block_rows, lanes), jnp.float32)
            for k in range(0, degree, step):
                lhs = jnp.concatenate([adj[b, k + i] for i in range(step)], axis=1)
                rhs = jnp.concatenate(sum([operand(p, s, b, k + i) for i in range(step)], []), axis=0)
                spread = spread + jnp.dot(lhs, rhs, preferred_element_type=jnp.float32)
            if s == 0:
                scale = jnp.broadcast_to(row_scale(p, b), (block_rows, lanes))
                scale_ref[here, :] = scale
            else:
                scale = scale_ref[here, :]
            labels = (ALPHA * spread + (1.0 - ALPHA) * anchor_ref[here, mine]) * scale
            if last:
                out_ref[here, mine] = labels
            else:
                keep(1 - p, s, b, labels)

        for q in range(CHUNKS):
            for j in range(1, pairs):
                far(p, s, j, q).wait_send()
                if width == 2:
                    forward(p, s, j, q).wait_send()
            if width == 2:
                near(p, s, q).wait_send()
        sent = reply.at[s, pl.ds(0, peers)]
        pltpu.make_async_copy(sent, sent, rep_send.at[p, s]).wait()
        if s == STREAMS - 1:
            for j in range(1, n_cols):
                sums_to(p, j).wait_send()
            sent = sums_reply.at[pl.ds(0, peers)]
            pltpu.make_async_copy(sent, sent, srep_send.at[p]).wait()

        if not last:
            if s == STREAMS - 1:
                start_sums(1 - p)
            start_gather(1 - p, s)

    start_sums(0)
    for s in range(STREAMS):
        start_gather(0, s)

    all_asked = asked_v.at[pl.ds(0, peers)]
    pltpu.make_async_copy(all_asked, all_asked, asked_recv).wait()
    pltpu.make_async_copy(all_asked, all_asked, asked_send).wait()
    to_scalar = pltpu.make_async_copy(asked_v, asked_s, asked_copy)
    to_scalar.start()
    to_scalar.wait()

    relay_sums(0)
    for s in range(STREAMS):
        relay(0, s)
    adj_copy.wait()

    for h in range(HOPS):
        for s in range(STREAMS):
            finish(h, s)
            if h < HOPS - 1:
                if s == STREAMS - 1:
                    relay_sums((h + 1) % 2)
                relay((h + 1) % 2, s)


def local(adjacency_tiles, col_block, label_prior, seed_label, seed_mask):
    blocks_dev, degree, block_rows, _ = adjacency_tiles.shape
    nodes, classes = label_prior.shape
    n_rows = lax.axis_size("rows")
    n_cols = lax.axis_size("cols")
    group = n_cols * blocks_dev
    lanes = classes // STREAMS
    padded = -(-n_rows // LANES) * LANES
    pairs = max(n_cols // 2 if n_cols % 2 == 0 else n_cols, 2)
    others = max(n_cols - 1, 1)
    unit = block_rows // sum(CHUNK_PARTS)
    dma = pltpu.SemaphoreType.DMA
    vmem = pl.BlockSpec(memory_space=pltpu.VMEM)
    return pl.pallas_call(
        functools.partial(kernel, n_rows, n_cols, blocks_dev, degree, block_rows, classes),
        out_shape=jax.ShapeDtypeStruct((nodes, classes), jnp.float32),
        in_specs=[
            pl.BlockSpec(memory_space=pl.ANY),
        ] * 5,
        out_specs=vmem,
        scratch_shapes=[
            [
                [
                    [
                        pltpu.VMEM((group + n_rows, unit * part, lanes), jnp.bfloat16)
                        for part in CHUNK_PARTS
                    ]
                    for _ in range(STREAMS)
                ]
                for _ in range(2)
            ],
            pltpu.VMEM((2, STREAMS, n_rows, block_rows, lanes), jnp.bfloat16),
            pltpu.VMEM((STREAMS, n_rows, block_rows, lanes), jnp.bfloat16),
            [pltpu.VMEM((group + n_rows, 1, block_rows), jnp.float32) for _ in range(2)],
            pltpu.VMEM((2, n_rows, 1, block_rows), jnp.float32),
            pltpu.VMEM((n_rows, 1, block_rows), jnp.float32),
            pltpu.VMEM((blocks_dev, 1, block_rows), jnp.float32),
            pltpu.VMEM((nodes, lanes), jnp.float32),
            pltpu.VMEM(adjacency_tiles.shape, jnp.bfloat16),
            pltpu.VMEM((nodes, classes), jnp.float32),
            pltpu.SMEM((blocks_dev * degree,), jnp.int32),
            pltpu.VMEM((1, padded), jnp.int32),
            pltpu.VMEM((n_rows, 1, padded), jnp.int32),
            pltpu.SMEM((n_rows, 1, padded), jnp.int32),
            pltpu.SMEM(col_block.shape, jnp.int32),
            pltpu.VMEM((nodes, classes), jnp.float32),
            pltpu.VMEM((blocks_dev, block_rows), jnp.int32),
            pltpu.VMEM((blocks_dev, block_rows), jnp.int32),
            dma((4,)),
            dma, dma, dma, dma,
            dma((2, STREAMS, CHUNKS)), dma((2, STREAMS, CHUNKS)),
            dma((2, STREAMS, pairs - 1, CHUNKS)), dma((2, STREAMS, pairs - 1, CHUNKS)),
            dma((2, STREAMS, pairs - 1, CHUNKS)), dma((2, STREAMS, pairs - 1, CHUNKS)),
            dma((2, STREAMS)), dma((2, STREAMS)),
            dma((2, others)), dma((2, others)),
            dma((2,)), dma((2,)),
        ],
        compiler_params=pltpu.CompilerParams(
            collective_id=0, has_side_effects=True, vmem_limit_bytes=VMEM_LIMIT - 4 * nodes * classes - SPARE
        ),
    )(
        col_block,
        label_prior,
        seed_label.reshape(blocks_dev, block_rows),
        seed_mask.reshape(blocks_dev, block_rows),
        adjacency_tiles,
    )


def solution(mesh):
    in_specs = (
        P(("rows", "cols"), None, None, None),
        P(("rows", "cols"), None),
        P(("rows", "cols"), None),
        P(("rows", "cols")),
        P(("rows", "cols")),
    )
    out_specs = P(("rows", "cols"), None)
    return jax.shard_map(local, mesh=mesh, in_specs=in_specs, out_specs=out_specs, check_vma=False)
```

time: 85.7 us -> 85 us (level)
  no operation moved by 1% of the time
where the time goes in v1:
time: 85 us; the launch traced here: 84.8 us
  Pallas kernels  82.7 us (97%)
  local copies, waits for them, and re-layouts  2.06 us (2%)
    pallas_call x1, Pallas kernels, local(): pl.pallas_call(functools.partial(kernel, n_rows, n_cols, blocks_dev, degr...  82.7 us
    unnamed x1, local copies, waits for them, and re-layouts  2.06 us

profile of v1, /device:TPU:0, one launch (start us, length us, event | category | flops | bytes accessed | tf_op | source)
XLA Modules:
  0.0 84.8 jit_solution(16354295154164818605)
XLA Ops:
  0.0 82.7 %shard_map.55 = f32[768,256]{1,0:T(8,128)} custom-call(s32[6,12]{1,0:T(8,128)} %col_block_hbm.1, f32[768,256]{1,0:T(8,128)} %prior_hbm.1, s32[6,128]{1,0:T(8,128)} %bitcast.2, s32[6,128]{1,0:T(8,128)} %bitcast.3, bf16[6,12,128,128]{3,2,1,0:T(8,128)(2,1)} %adj_hbm.1), custom_call_target="tpu_custom_call" | custom-call | tf_op jit(solution)/shard_map/pallas_call | solution.py:336
  82.8 2.1 %copy.7 = f32[768,256]{1,0:T(8,128)} copy(f32[768,256]{1,0:T(8,128)} %shard_map.55) | data formatting | bytes 1572864

commit v2 on v1

v2 whole, which is shorter than its diff:
```python
import functools

import jax
import jax.numpy as jnp
from jax import lax
from jax.experimental import pallas as pl
from jax.experimental.pallas import tpu as pltpu
from jax.sharding import PartitionSpec as P

HOPS = 4
STREAMS = 2
CHUNK_PARTS = (2, 2, 4)
HEAD = "S G0 G1 G2".split()
EARLY = "U A0 A1".split()
LATE = "A2".split()
CHUNKS = len(CHUNK_PARTS)
ALPHA = 0.85
SEED_BOOST = 8.0
LANES = 128
VMEM_LIMIT = 67_043_328
SPARE = 64 * 1024
MESH = pl.DeviceIdType.MESH


def kernel(
    n_rows, n_cols, blocks_dev, degree, block_rows, classes,
    col_block_hbm, prior_hbm, label_hbm, mask_hbm, adj_hbm, out_ref,
    tables, remote, reply, landed, sums, sums_remote, sums_reply, sums_part, scale_ref, blend_ref,
    adj, anchor_ref, index_ref, wanted_ref, asked_v, asked_s,
    col_block_ref, prior_ref, label_ref, mask_ref, in_sem,
    adj_sem, asked_send, asked_recv, asked_copy,
    near_send, near_recv, far_send, far_recv, fwd_send, fwd_recv, rep_send, rep_recv,
    sums_send, sums_recv, srep_send, srep_recv,
):
    row = lax.axis_index("rows")
    col = lax.axis_index("cols")
    group = n_cols * blocks_dev
    lanes = classes // STREAMS
    pairs = n_cols // 2
    pair, low = col // 2, col % 2
    mate = pair * 2 + 1 - low
    unit = block_rows // sum(CHUNK_PARTS)
    starts = [unit * sum(CHUNK_PARTS[:q]) for q in range(CHUNKS)]
    sizes = [unit * part for part in CHUNK_PARTS]
    halves = [size // 2 for size in sizes]
    peers = n_rows - 1

    def each_peer(body):
        half = n_rows // 2
        def step(i):
            if isinstance(i, int):
                d = half + ((i + 1) // 2) * (1 - 2 * (i % 2))
            else:
                d = half + lax.div(i + 1, 2) * (1 - 2 * lax.rem(i, 2))
            body((row + d + n_rows) % n_rows)
        if n_rows <= 8:
            for i in range(peers):
                step(i)
        else:
            def loop(i, carry):
                step(i)
                return carry
            lax.fori_loop(0, peers, loop, 0)

    adj_copy = pltpu.make_async_copy(adj_hbm, adj, adj_sem)
    loads = [
        pltpu.make_async_copy(source, target, in_sem.at[i])
        for i, (source, target) in enumerate([
            (col_block_hbm, col_block_ref),
            (label_hbm, label_ref),
            (mask_hbm, mask_ref),
            (prior_hbm, prior_ref),
        ])
    ]
    for load in loads:
        load.start()
    adj_copy.start()

    barrier = pltpu.get_barrier_semaphore()
    for j in range(1, n_cols):
        pl.semaphore_signal(
            barrier, inc=1, device_id=(row, (col + j) % n_cols), device_id_type=MESH
        )
    def greet(other):
        for r in range(2):
            pl.semaphore_signal(
                barrier, inc=1, device_id=(other, pair * 2 + r), device_id_type=MESH
            )

    each_peer(greet)

    ones = jnp.ones((8, lanes), jnp.bfloat16)

    def keep(p, s, b, labels):
        sent = labels.astype(jnp.bfloat16)
        for q in range(CHUNKS):
            tables[p][s][q][col * blocks_dev + b] = sent[starts[q] : starts[q] + sizes[q], :]

    def sum_rows(p, s):
        for b in range(blocks_dev):
            mine = col * blocks_dev + b
            sent = jnp.concatenate([tables[p][s][q][mine] for q in range(CHUNKS)], axis=0)
            total = lax.dot_general(
                ones, sent, (((1,), (1,)), ((), ())), preferred_element_type=jnp.float32
            )[:1, :]
            if s > 0:
                total = total + sums_part[b]
            if s < STREAMS - 1:
                sums_part[b] = total
            else:
                sums[p][mine] = total

    loads[0].wait()
    lane = lax.broadcasted_iota(jnp.int32, wanted_ref.shape, 1)
    wanted = jnp.zeros(wanted_ref.shape, jnp.int32)
    for b in range(blocks_dev):
        for k in range(degree):
            block = col_block_ref[b, k]
            owner = lax.div(block, group)
            within = block - owner * group
            index_ref[b * degree + k] = jnp.where(owner == row, within, group + owner)
            wanted = jnp.where(lane == owner, within, wanted)
    wanted_ref[...] = wanted

    pl.semaphore_wait(barrier, n_cols - 1 + 2 * peers)

    def send_wanted(other):
        for r in range(2):
            pltpu.make_async_remote_copy(
                src_ref=wanted_ref, dst_ref=asked_v.at[low, row],
                send_sem=asked_send, recv_sem=asked_recv,
                device_id=(other, pair * 2 + r), device_id_type=MESH,
            ).start()

    each_peer(send_wanted)

    for load in loads[1:]:
        load.wait()
    code = jnp.where(mask_ref[...] > 0, label_ref[...], -1)
    for b in range(blocks_dev):
        here = slice(b * block_rows, (b + 1) * block_rows)
        across = jnp.broadcast_to(code[b : b + 1, :], (block_rows, block_rows)).T
        class_id = lax.broadcasted_iota(jnp.int32, (block_rows, classes), 1)
        across = jnp.concatenate([across] * (classes // block_rows), axis=1)
        raw = prior_ref[here, :] + jnp.where(class_id == across, SEED_BOOST, 0.0)
        anchor = raw * (classes / jnp.sum(raw, axis=1, keepdims=True))
        anchor_ref[here, :] = anchor
        for s in range(STREAMS):
            keep(0, s, b, anchor[:, s * lanes : (s + 1) * lanes])

    def rows_of(q, r):
        return pl.ds(pl.multiple_of(r * halves[q], 16), halves[q])

    def near(p, s, q):
        ref = tables[p][s][q].at[pl.ds(col * blocks_dev, blocks_dev)]
        return pltpu.make_async_remote_copy(
            src_ref=ref, dst_ref=ref,
            send_sem=near_send.at[p, s, q], recv_sem=near_recv.at[p, s, q],
            device_id=(row, mate), device_id_type=MESH,
        )

    def far(p, s, j, q, d):
        r = (low + d) % 2
        ref = tables[p][s][q].at[pl.ds(col * blocks_dev, blocks_dev), rows_of(q, r), :]
        return pltpu.make_async_remote_copy(
            src_ref=ref, dst_ref=ref,
            send_sem=far_send.at[p, s, j - 1, q, d], recv_sem=far_recv.at[p, s, j - 1, q, d],
            device_id=(row, ((pair + j) % pairs) * 2 + r), device_id_type=MESH,
        )

    def forward(p, s, j, q):
        first = ((pair + pairs - j) % pairs) * 2 * blocks_dev
        return pltpu.make_async_remote_copy(
            src_ref=tables[p][s][q].at[pl.ds(first, 2 * blocks_dev), rows_of(q, low), :],
            dst_ref=landed[p][s][q].at[pl.ds((j - 1) * 2 * blocks_dev, 2 * blocks_dev)],
            send_sem=fwd_send.at[p, s, j - 1, q], recv_sem=fwd_recv.at[p, s, j - 1, q],
            device_id=(row, mate), device_id_type=MESH,
        )

    def sums_to(p, j):
        ref = sums[p].at[pl.ds(col * blocks_dev, blocks_dev)]
        return pltpu.make_async_remote_copy(
            src_ref=ref, dst_ref=ref,
            send_sem=sums_send.at[p, j - 1], recv_sem=sums_recv.at[p, j - 1],
            device_id=(row, (col + j) % n_cols), device_id_type=MESH,
        )

    def start_sums(p):
        for j in range(1, n_cols):
            sums_to(p, j).start()

    def start_gather(p, s, q):
        for j in range(1, pairs):
            for d in range(2):
                far(p, s, j, q, d).start()
        near(p, s, q).start()

    def relay_sums(p):
        for j in range(1, n_cols):
            sums_to(p, j).wait_recv()

        def answer(other):
            sums_reply[other] = sums[p][asked_s[low, other, 0, row]]
            pltpu.make_async_remote_copy(
                src_ref=sums_reply.at[other], dst_ref=sums_remote.at[p, row],
                send_sem=srep_send.at[p], recv_sem=srep_recv.at[p],
                device_id=(other, col), device_id_type=MESH,
            ).start()

        each_peer(answer)

    def relay(p, s, steps):
        for kind, q in [(text[0], int(text[1:] or 0)) for text in steps]:
            if kind == "G":
                start_gather(p, s, q)
                continue
            if kind == "S":
                sum_rows(p, s)
                if s == STREAMS - 1:
                    start_sums(p)
                continue
            if kind == "U":
                if s == STREAMS - 1:
                    relay_sums(p)
                continue
            for j in range(1, pairs):
                for d in range(2):
                    far(p, s, j, q, d).wait_recv()
            near(p, s, q).wait_recv()
            rows_q = pl.ds(pl.multiple_of(starts[q] + low * halves[q], 16), halves[q])

            def answer(other):
                for r in range(2):
                    reply[s, r, other, rows_q, :] = tables[p][s][q][
                        asked_s[r, other, 0, row], rows_of(q, low), :
                    ]
                    pltpu.make_async_remote_copy(
                        src_ref=reply.at[s, r, other, rows_q, :],
                        dst_ref=remote.at[p, s, row, rows_q, :],
                        send_sem=rep_send.at[p, s], recv_sem=rep_recv.at[p, s],
                        device_id=(other, pair * 2 + r), device_id_type=MESH,
                    ).start()

            each_peer(answer)
            for j in range(1, pairs):
                forward(p, s, j, q).start()

    def operand(p, s, b, k):
        index = index_ref[b * degree + k]
        return [tables[p][s][q][index] for q in range(CHUNKS)]

    def row_scale(p, b):
        here = slice(b * block_rows, (b + 1) * block_rows)
        total = jnp.zeros((block_rows, block_rows), jnp.float32)
        for k in range(degree):
            total = total + adj[b, k].astype(jnp.float32) * sums[p][index_ref[b * degree + k]]
        rest = anchor_ref[here, :block_rows]
        for i in range(1, classes // block_rows):
            rest = rest + anchor_ref[here, i * block_rows : (i + 1) * block_rows]
        total = ALPHA * total + (1.0 - ALPHA) * rest
        return classes / jnp.sum(total, axis=1, keepdims=True)

    def finish(h, s):
        p, last = h % 2, h == HOPS - 1
        got = remote.at[p, s, pl.ds(0, peers)]
        pltpu.make_async_copy(got, got, rep_recv.at[p, s]).wait()

        for q in range(CHUNKS):
            for j in range(1, pairs):
                forward(p, s, j, q).wait_recv()
                first = ((pair + pairs - j) % pairs) * 2 * blocks_dev
                tables[p][s][q][pl.ds(first, 2 * blocks_dev), rows_of(q, 1 - low), :] = landed[p][s][q][
                    pl.ds((j - 1) * 2 * blocks_dev, 2 * blocks_dev)
                ]

        def fold(other):
            for q in range(CHUNKS):
                tables[p][s][q][group + other] = remote[p, s, other, pl.ds(starts[q], sizes[q]), :]

        each_peer(fold)

        step = 2 if degree % 2 == 0 else 1
        mine = slice(s * lanes, (s + 1) * lanes)

        def blend(b):
            here = slice(b * block_rows, (b + 1) * block_rows)
            spread = jnp.zeros((block_rows, lanes), jnp.float32)
            for k in range(0, degree, step):
                lhs = jnp.concatenate([adj[b, k + i] for i in range(step)], axis=1)
                rhs = jnp.concatenate(sum([operand(p, s, b, k + i) for i in range(step)], []), axis=0)
                spread = spread + jnp.dot(lhs, rhs, preferred_element_type=jnp.float32)
            return ALPHA * spread + (1.0 - ALPHA) * anchor_ref[here, mine]

        if s == 0:
            for b in range(blocks_dev):
                blend_ref[b * block_rows : (b + 1) * block_rows, :] = blend(b)
            got = sums_remote.at[p, pl.ds(0, peers)]
            pltpu.make_async_copy(got, got, srep_recv.at[p]).wait()

            def fold_sums(other):
                sums[p][group + other] = sums_remote[p, other]

            each_peer(fold_sums)

        for b in range(blocks_dev):
            here = slice(b * block_rows, (b + 1) * block_rows)
            if s == 0:
                scale = jnp.broadcast_to(row_scale(p, b), (block_rows, lanes))
                scale_ref[here, :] = scale
                labels = blend_ref[here, :] * scale
            else:
                labels = blend(b) * scale_ref[here, :]
            if last:
                out_ref[here, mine] = labels
            else:
                keep(1 - p, s, b, labels)

        for q in range(CHUNKS):
            for j in range(1, pairs):
                for d in range(2):
                    far(p, s, j, q, d).wait_send()
                forward(p, s, j, q).wait_send()
            near(p, s, q).wait_send()
        for r in range(2):
            sent = reply.at[s, r, pl.ds(0, peers), pl.ds(0, block_rows // 2), :]
            pltpu.make_async_copy(sent, sent, rep_send.at[p, s]).wait()
        if s == STREAMS - 1:
            for j in range(1, n_cols):
                sums_to(p, j).wait_send()
            sent = sums_reply.at[pl.ds(0, peers)]
            pltpu.make_async_copy(sent, sent, srep_send.at[p]).wait()


    for s in range(STREAMS):
        relay(0, s, ["S"])
    for s in range(STREAMS):
        relay(0, s, HEAD[1:])

    all_asked = asked_v.at[:, pl.ds(0, peers)]
    pltpu.make_async_copy(all_asked, all_asked, asked_recv).wait()
    pltpu.make_async_copy(all_asked, all_asked, asked_send).wait()
    to_scalar = pltpu.make_async_copy(asked_v, asked_s, asked_copy)
    to_scalar.start()
    to_scalar.wait()

    relay_sums(0)
    for s in range(STREAMS):
        relay(0, s, EARLY[1:])
        if s < STREAMS - 1:
            relay(0, s, LATE)
    adj_copy.wait()
    left = (0, STREAMS - 1)

    for h in range(HOPS):
        p = (h + 1) % 2
        for s in range(STREAMS):
            finish(h, s)
            if h < HOPS - 1:
                relay(p, s, HEAD)
            if left is not None:
                relay(*left, LATE)
                left = None
            if h < HOPS - 1:
                relay(p, s, EARLY)
                left = (p, s)
                if h == HOPS - 2 and s == STREAMS - 1:
                    relay(p, s, LATE)
                    left = None


def local(adjacency_tiles, col_block, label_prior, seed_label, seed_mask):
    blocks_dev, degree, block_rows, _ = adjacency_tiles.shape
    nodes, classes = label_prior.shape
    n_rows = lax.axis_size("rows")
    n_cols = lax.axis_size("cols")
    group = n_cols * blocks_dev
    lanes = classes // STREAMS
    padded = -(-n_rows // LANES) * LANES
    pairs = max(n_cols // 2, 2)
    span = (pairs - 1) * 2 * blocks_dev
    others = max(n_cols - 1, 1)
    unit = block_rows // sum(CHUNK_PARTS)
    dma = pltpu.SemaphoreType.DMA
    vmem = pl.BlockSpec(memory_space=pltpu.VMEM)
    return pl.pallas_call(
        functools.partial(kernel, n_rows, n_cols, blocks_dev, degree, block_rows, classes),
        out_shape=jax.ShapeDtypeStruct((nodes, classes), jnp.float32),
        in_specs=[
            pl.BlockSpec(memory_space=pl.ANY),
        ] * 5,
        out_specs=vmem,
        scratch_shapes=[
            [
                [
                    [
                        pltpu.VMEM((group + n_rows, unit * part, lanes), jnp.bfloat16)
                        for part in CHUNK_PARTS
                    ]
                    for _ in range(STREAMS)
                ]
                for _ in range(2)
            ],
            pltpu.VMEM((2, STREAMS, n_rows, block_rows, lanes), jnp.bfloat16),
            pltpu.VMEM((STREAMS, 2, n_rows, block_rows, lanes), jnp.bfloat16),
            [
                [
                    [pltpu.VMEM((span, unit * part // 2, lanes), jnp.bfloat16) for part in CHUNK_PARTS]
                    for _ in range(STREAMS)
                ]
                for _ in range(2)
            ],
            [pltpu.VMEM((group + n_rows, 1, block_rows), jnp.float32) for _ in range(2)],
            pltpu.VMEM((2, n_rows, 1, block_rows), jnp.float32),
            pltpu.VMEM((n_rows, 1, block_rows), jnp.float32),
            pltpu.VMEM((blocks_dev, 1, block_rows), jnp.float32),
            pltpu.VMEM((nodes, lanes), jnp.float32),
            pltpu.VMEM((nodes, lanes), jnp.float32),
            pltpu.VMEM(adjacency_tiles.shape, jnp.bfloat16),
            pltpu.VMEM((nodes, classes), jnp.float32),
            pltpu.SMEM((blocks_dev * degree,), jnp.int32),
            pltpu.VMEM((1, padded), jnp.int32),
            pltpu.VMEM((2, n_rows, 1, padded), jnp.int32),
            pltpu.SMEM((2, n_rows, 1, padded), jnp.int32),
            pltpu.SMEM(col_block.shape, jnp.int32),
            pltpu.VMEM((nodes, classes), jnp.float32),
            pltpu.VMEM((blocks_dev, block_rows), jnp.int32),
            pltpu.VMEM((blocks_dev, block_rows), jnp.int32),
            dma((4,)),
            dma, dma, dma, dma,
            dma((2, STREAMS, CHUNKS)), dma((2, STREAMS, CHUNKS)),
            dma((2, STREAMS, pairs - 1, CHUNKS, 2)), dma((2, STREAMS, pairs - 1, CHUNKS, 2)),
            dma((2, STREAMS, pairs - 1, CHUNKS)), dma((2, STREAMS, pairs - 1, CHUNKS)),
            dma((2, STREAMS)), dma((2, STREAMS)),
            dma((2, others)), dma((2, others)),
            dma((2,)), dma((2,)),
        ],
        compiler_params=pltpu.CompilerParams(
            collective_id=0, has_side_effects=True, vmem_limit_bytes=VMEM_LIMIT - 4 * nodes * classes - SPARE
        ),
    )(
        col_block,
        label_prior,
        seed_label.reshape(blocks_dev, block_rows),
        seed_mask.reshape(blocks_dev, block_rows),
        adjacency_tiles,
    )


def solution(mesh):
    in_specs = (
        P(("rows", "cols"), None, None, None),
        P(("rows", "cols"), None),
        P(("rows", "cols"), None),
        P(("rows", "cols")),
        P(("rows", "cols")),
    )
    out_specs = P(("rows", "cols"), None)
    return jax.shard_map(local, mesh=mesh, in_specs=in_specs, out_specs=out_specs, check_vma=False)
```

time: 85 us -> 71.6 us (0.84)
  Pallas kernels: 82.7 us -> 69.3 us
    pallas_call x1, Pallas kernels: 82.7 us -> 69.3 us  [local(): pl.pallas_call(functools.partial(kernel, n_rows, n_cols, blocks_dev, degr...]
where the time goes in v2:
time: 71.6 us; the launch traced here: 71.4 us
  Pallas kernels  69.3 us (97%)
  local copies, waits for them, and re-layouts  2.06 us (3%)
    pallas_call x1, Pallas kernels, local(): pl.pallas_call(functools.partial(kernel, n_rows, n_cols, blocks_dev, degr...  69.3 us
    unnamed x1, local copies, waits for them, and re-layouts  2.06 us

profile of v2, /device:TPU:0, one launch (start us, length us, event | category | flops | bytes accessed | tf_op | source)
XLA Modules:
  0.0 71.4 jit_solution(16071709858518518609)
XLA Ops:
  0.0 69.3 %shard_map.55 = f32[768,256]{1,0:T(8,128)} custom-call(s32[6,12]{1,0:T(8,128)} %col_block_hbm.1, f32[768,256]{1,0:T(8,128)} %prior_hbm.1, s32[6,128]{1,0:T(8,128)} %bitcast.2, s32[6,128]{1,0:T(8,128)} %bitcast.3, bf16[6,12,128,128]{3,2,1,0:T(8,128)(2,1)} %adj_hbm.1), custom_call_target="tpu_custom_call" | custom-call | tf_op jit(solution)/shard_map/pallas_call | solution.py:385
  69.3 2.1 %copy.7 = f32[768,256]{1,0:T(8,128)} copy(f32[768,256]{1,0:T(8,128)} %shard_map.55) | data formatting | bytes 1572864

commit v3 on v2

--- a/solution.py
+++ b/solution.py
@@ -10,22 +10,24 @@
 HOPS = 4
 STREAMS = 2
 CHUNK_PARTS = (2, 2, 4)
-HEAD = "S G0 G1 G2".split()
-EARLY = "U A0 A1".split()
+EARLY = "A0 A1".split()
 LATE = "A2".split()
+BETWEEN = ("M0 M1 A0 A1".split(), "U M0 A0 M1 A1".split())
 CHUNKS = len(CHUNK_PARTS)
+HEAD = [f"G{q}" for q in range(CHUNKS)]
 ALPHA = 0.85
 SEED_BOOST = 8.0
 LANES = 128
 VMEM_LIMIT = 67_043_328
 SPARE = 64 * 1024
 MESH = pl.DeviceIdType.MESH
+PEER_ORDER = (5, 4, 7, 6, 3, 2, 1)
 
 
 def kernel(
     n_rows, n_cols, blocks_dev, degree, block_rows, classes,
     col_block_hbm, prior_hbm, label_hbm, mask_hbm, adj_hbm, out_ref,
-    tables, remote, reply, landed, sums, sums_remote, sums_reply, sums_part, scale_ref, blend_ref,
+    tables, remote, reply, landed, sums, sums_remote, sums_reply, sums_part, scale_ref, blend_ref, adj_q,
     adj, anchor_ref, index_ref, wanted_ref, asked_v, asked_s,
     col_block_ref, prior_ref, label_ref, mask_ref, in_sem,
     adj_sem, asked_send, asked_recv, asked_copy,
@@ -46,6 +48,15 @@
     peers = n_rows - 1
 
     def each_peer(body):
+        if n_rows <= 8 and n_rows & (n_rows - 1) == 0:
+            for flips in PEER_ORDER:
+                if flips < n_rows:
+                    other = row
+                    for i in range(3):
+                        if flips >> i & 1:
+                            other = other + (1 << i) * (1 - 2 * ((row // (1 << i)) % 2))
+                    body(other)
+            return
         half = n_rows // 2
         def step(i):
             if isinstance(i, int):
@@ -149,7 +160,7 @@
             keep(0, s, b, anchor[:, s * lanes : (s + 1) * lanes])
 
     def rows_of(q, r):
-        return pl.ds(pl.multiple_of(r * halves[q], 16), halves[q])
+        return pl.ds(pl.multiple_of(r * halves[q], 8), halves[q])
 
     def near(p, s, q):
         ref = tables[p][s][q].at[pl.ds(col * blocks_dev, blocks_dev)]
@@ -227,7 +238,7 @@
                 for d in range(2):
                     far(p, s, j, q, d).wait_recv()
             near(p, s, q).wait_recv()
-            rows_q = pl.ds(pl.multiple_of(starts[q] + low * halves[q], 16), halves[q])
+            rows_q = pl.ds(pl.multiple_of(starts[q] + low * halves[q], 8), halves[q])
 
             def answer(other):
                 for r in range(2):
@@ -237,7 +248,7 @@
                     pltpu.make_async_remote_copy(
                         src_ref=reply.at[s, r, other, rows_q, :],
                         dst_ref=remote.at[p, s, row, rows_q, :],
-                        send_sem=rep_send.at[p, s], recv_sem=rep_recv.at[p, s],
+                        send_sem=rep_send.at[p, s], recv_sem=rep_recv.at[p, s, q],
                         device_id=(other, pair * 2 + r), device_id_type=MESH,
                     ).start()
 
@@ -245,9 +256,11 @@
             for j in range(1, pairs):
                 forward(p, s, j, q).start()
 
-    def operand(p, s, b, k):
-        index = index_ref[b * degree + k]
-        return [tables[p][s][q][index] for q in range(CHUNKS)]
+    def product(p, s, b, q):
+        rhs = [tables[p][s][q][index_ref[b * degree + k]] for k in range(degree)]
+        return jnp.dot(
+            adj_q[q][b], jnp.concatenate(rhs, axis=0), preferred_element_type=jnp.float32
+        )
 
     def row_scale(p, b):
         here = slice(b * block_rows, (b + 1) * block_rows)
@@ -260,40 +273,50 @@
         total = ALPHA * total + (1.0 - ALPHA) * rest
         return classes / jnp.sum(total, axis=1, keepdims=True)
 
+    def blend(p, s, b, q, mine):
+        here = slice(b * block_rows, (b + 1) * block_rows)
+        spread = product(p, s, b, q)
+        if q > 0:
+            spread = spread + blend_ref[s, here, :]
+        if q < CHUNKS - 1:
+            return spread
+        return ALPHA * spread + (1.0 - ALPHA) * anchor_ref[here, mine]
+
+    blended = {}
+
+    def gathered(p, s, q):
+        rows_q = pl.ds(starts[q], sizes[q])
+        got = remote.at[p, s, pl.ds(0, peers), rows_q, :]
+        pltpu.make_async_copy(got, got, rep_recv.at[p, s, q]).wait()
+        for j in range(1, pairs):
+            forward(p, s, j, q).wait_recv()
+            first = ((pair + pairs - j) % pairs) * 2 * blocks_dev
+            tables[p][s][q][pl.ds(first, 2 * blocks_dev), rows_of(q, 1 - low), :] = landed[p][s][q][
+                pl.ds((j - 1) * 2 * blocks_dev, 2 * blocks_dev)
+            ]
+
+        def fold(other):
+            tables[p][s][q][group + other] = remote[p, s, other, rows_q, :]
+
+        each_peer(fold)
+
+    def partial(h, s, q):
+        p = h % 2
+        gathered(p, s, q)
+        for b in range(blocks_dev):
+            here = slice(b * block_rows, (b + 1) * block_rows)
+            blend_ref[s, here, :] = blend(p, s, b, q, slice(s * lanes, (s + 1) * lanes))
+        blended[h, s] = q + 1
+
     def finish(h, s):
         p, last = h % 2, h == HOPS - 1
-        got = remote.at[p, s, pl.ds(0, peers)]
-        pltpu.make_async_copy(got, got, rep_recv.at[p, s]).wait()
-
-        for q in range(CHUNKS):
-            for j in range(1, pairs):
-                forward(p, s, j, q).wait_recv()
-                first = ((pair + pairs - j) % pairs) * 2 * blocks_dev
-                tables[p][s][q][pl.ds(first, 2 * blocks_dev), rows_of(q, 1 - low), :] = landed[p][s][q][
-                    pl.ds((j - 1) * 2 * blocks_dev, 2 * blocks_dev)
-                ]
-
-        def fold(other):
-            for q in range(CHUNKS):
-                tables[p][s][q][group + other] = remote[p, s, other, pl.ds(starts[q], sizes[q]), :]
-
-        each_peer(fold)
-
-        step = 2 if degree % 2 == 0 else 1
         mine = slice(s * lanes, (s + 1) * lanes)
-
-        def blend(b):
-            here = slice(b * block_rows, (b + 1) * block_rows)
-            spread = jnp.zeros((block_rows, lanes), jnp.float32)
-            for k in range(0, degree, step):
-                lhs = jnp.concatenate([adj[b, k + i] for i in range(step)], axis=1)
-                rhs = jnp.concatenate(sum([operand(p, s, b, k + i) for i in range(step)], []), axis=0)
-                spread = spread + jnp.dot(lhs, rhs, preferred_element_type=jnp.float32)
-            return ALPHA * spread + (1.0 - ALPHA) * anchor_ref[here, mine]
+        for q in range(blended.get((h, s), 0), CHUNKS - (s > 0)):
+            partial(h, s, q)
+        if s > 0:
+            gathered(p, s, CHUNKS - 1)
 
         if s == 0:
-            for b in range(blocks_dev):
-                blend_ref[b * block_rows : (b + 1) * block_rows, :] = blend(b)
             got = sums_remote.at[p, pl.ds(0, peers)]
             pltpu.make_async_copy(got, got, srep_recv.at[p]).wait()
 
@@ -307,9 +330,9 @@
             if s == 0:
                 scale = jnp.broadcast_to(row_scale(p, b), (block_rows, lanes))
                 scale_ref[here, :] = scale
-                labels = blend_ref[here, :] * scale
+                labels = blend_ref[s, here, :] * scale
             else:
-                labels = blend(b) * scale_ref[here, :]
+                labels = blend(p, s, b, CHUNKS - 1, mine) * scale_ref[here, :]
             if last:
                 out_ref[here, mine] = labels
             else:
@@ -334,7 +357,7 @@
     for s in range(STREAMS):
         relay(0, s, ["S"])
     for s in range(STREAMS):
-        relay(0, s, HEAD[1:])
+        relay(0, s, HEAD)
 
     all_asked = asked_v.at[:, pl.ds(0, peers)]
     pltpu.make_async_copy(all_asked, all_asked, asked_recv).wait()
@@ -345,10 +368,14 @@
 
     relay_sums(0)
     for s in range(STREAMS):
-        relay(0, s, EARLY[1:])
+        relay(0, s, EARLY)
         if s < STREAMS - 1:
             relay(0, s, LATE)
     adj_copy.wait()
+    for b in range(blocks_dev):
+        for q in range(CHUNKS):
+            columns = slice(starts[q], starts[q] + sizes[q])
+            adj_q[q][b] = jnp.concatenate([adj[b, k][:, columns] for k in range(degree)], axis=1)
     left = (0, STREAMS - 1)
 
     for h in range(HOPS):
@@ -356,12 +383,17 @@
         for s in range(STREAMS):
             finish(h, s)
             if h < HOPS - 1:
-                relay(p, s, HEAD)
+                relay(p, s, ["S"] + HEAD if s == STREAMS - 1 else HEAD + ["S"])
             if left is not None:
                 relay(*left, LATE)
                 left = None
             if h < HOPS - 1:
-                relay(p, s, EARLY)
+                pending = (h, s + 1) if s < STREAMS - 1 else (h + 1, 0)
+                for text in BETWEEN[s > 0]:
+                    if text[0] == "M":
+                        partial(*pending, int(text[1:]))
+                    else:
+                        relay(p, s, [text])
                 left = (p, s)
                 if h == HOPS - 2 and s == STREAMS - 1:
                     relay(p, s, LATE)
@@ -414,7 +446,11 @@
             pltpu.VMEM((n_rows, 1, block_rows), jnp.float32),
             pltpu.VMEM((blocks_dev, 1, block_rows), jnp.float32),
             pltpu.VMEM((nodes, lanes), jnp.float32),
-            pltpu.VMEM((nodes, lanes), jnp.float32),
+            pltpu.VMEM((STREAMS, nodes, lanes), jnp.float32),
+            [
+                pltpu.VMEM((blocks_dev, block_rows, degree * unit * part), jnp.bfloat16)
+                for part in CHUNK_PARTS
+            ],
             pltpu.VMEM(adjacency_tiles.shape, jnp.bfloat16),
             pltpu.VMEM((nodes, classes), jnp.float32),
             pltpu.SMEM((blocks_dev * degree,), jnp.int32),
@@ -430,7 +466,7 @@
             dma((2, STREAMS, CHUNKS)), dma((2, STREAMS, CHUNKS)),
             dma((2, STREAMS, pairs - 1, CHUNKS, 2)), dma((2, STREAMS, pairs - 1, CHUNKS, 2)),
             dma((2, STREAMS, pairs - 1, CHUNKS)), dma((2, STREAMS, pairs - 1, CHUNKS)),
-            dma((2, STREAMS)), dma((2, STREAMS)),
+            dma((2, STREAMS)), dma((2, STREAMS, CHUNKS)),
             dma((2, others)), dma((2, others)),
             dma((2,)), dma((2,)),
         ],

time: 71.6 us -> 68.8 us (0.961)
  Pallas kernels: 69.3 us -> 66.6 us
    pallas_call x1, Pallas kernels: 69.3 us -> 66.6 us  [local(): pl.pallas_call(functools.partial(kernel, n_rows, n_cols, blocks_dev, degr...]
where the time goes in v3:
time: 68.8 us; the launch traced here: 68.7 us
  Pallas kernels  66.6 us (97%)
  local copies, waits for them, and re-layouts  2.06 us (3%)
    pallas_call x1, Pallas kernels, local(): pl.pallas_call(functools.partial(kernel, n_rows, n_cols, blocks_dev, degr...  66.6 us
    unnamed x1, local copies, waits for them, and re-layouts  2.06 us

profile of v3, /device:TPU:0, one launch (start us, length us, event | category | flops | bytes accessed | tf_op | source)
XLA Modules:
  0.0 68.7 jit_solution(389216070738856437)
XLA Ops:
  0.0 66.6 %shard_map.55 = f32[768,256]{1,0:T(8,128)} custom-call(s32[6,12]{1,0:T(8,128)} %col_block_hbm.1, f32[768,256]{1,0:T(8,128)} %prior_hbm.1, s32[6,128]{1,0:T(8,128)} %bitcast.2, s32[6,128]{1,0:T(8,128)} %bitcast.3, bf16[6,12,128,128]{3,2,1,0:T(8,128)(2,1)} %adj_hbm.1), custom_call_target="tpu_custom_call" | custom-call | tf_op jit(solution)/shard_map/pallas_call | solution.py:417
  66.6 2.1 %copy.7 = f32[768,256]{1,0:T(8,128)} copy(f32[768,256]{1,0:T(8,128)} %shard_map.55) | data formatting | bytes 1572864

commit v4 on v3

--- a/solution.py
+++ b/solution.py
@@ -10,9 +10,9 @@
 HOPS = 4
 STREAMS = 2
 CHUNK_PARTS = (2, 2, 4)
-EARLY = "A0 A1".split()
-LATE = "A2".split()
-BETWEEN = ("M0 M1 A0 A1".split(), "U M0 A0 M1 A1".split())
+EARLY = ("A0", "A1")
+LATE = ("A2",)
+BETWEEN = (("M0", "M1", "A0", "A1"), ("U", "M0", "A0", "M1", "A1"))
 CHUNKS = len(CHUNK_PARTS)
 HEAD = [f"G{q}" for q in range(CHUNKS)]
 ALPHA = 0.85
@@ -188,17 +188,34 @@
             device_id=(row, mate), device_id_type=MESH,
         )
 
-    def sums_to(p, j):
+    def sums_near(p):
+        ref = sums[p].at[pl.ds(col * blocks_dev, blocks_dev)]
+        return pltpu.make_async_remote_copy(
+            src_ref=ref, dst_ref=ref, send_sem=sums_send.at[p, 0], recv_sem=sums_recv.at[p, 0],
+            device_id=(row, mate), device_id_type=MESH,
+        )
+
+    def sums_far(p, j, d):
         ref = sums[p].at[pl.ds(col * blocks_dev, blocks_dev)]
         return pltpu.make_async_remote_copy(
             src_ref=ref, dst_ref=ref,
-            send_sem=sums_send.at[p, j - 1], recv_sem=sums_recv.at[p, j - 1],
-            device_id=(row, (col + j) % n_cols), device_id_type=MESH,
+            send_sem=sums_send.at[p, j], recv_sem=sums_recv.at[p, 2 * j - 1 + d],
+            device_id=(row, ((pair + j) % pairs) * 2 + 1), device_id_type=MESH,
+        )
+
+    def sums_forward(p, j):
+        first = ((pair + pairs - j) % pairs) * 2 * blocks_dev
+        ref = sums[p].at[pl.ds(first, 2 * blocks_dev)]
+        return pltpu.make_async_remote_copy(
+            src_ref=ref, dst_ref=ref,
+            send_sem=sums_send.at[p, pairs - 1 + j], recv_sem=sums_recv.at[p, 2 * (pairs - 1) + j],
+            device_id=(row, mate), device_id_type=MESH,
         )
 
     def start_sums(p):
-        for j in range(1, n_cols):
-            sums_to(p, j).start()
+        for j in range(1, pairs):
+            sums_far(p, j, low).start()
+        sums_near(p).start()
 
     def start_gather(p, s, q):
         for j in range(1, pairs):
@@ -207,18 +224,26 @@
         near(p, s, q).start()
 
     def relay_sums(p):
-        for j in range(1, n_cols):
-            sums_to(p, j).wait_recv()
-
-        def answer(other):
-            sums_reply[other] = sums[p][asked_s[low, other, 0, row]]
-            pltpu.make_async_remote_copy(
-                src_ref=sums_reply.at[other], dst_ref=sums_remote.at[p, row],
-                send_sem=srep_send.at[p], recv_sem=srep_recv.at[p],
-                device_id=(other, col), device_id_type=MESH,
-            ).start()
-
-        each_peer(answer)
+        sums_near(p).wait_recv()
+
+        @pl.when(low == 1)
+        def _():
+            for j in range(1, pairs):
+                for d in range(2):
+                    sums_far(p, j, d).wait_recv()
+
+            def answer(other):
+                for r in range(2):
+                    sums_reply[r, other] = sums[p][asked_s[r, other, 0, row]]
+                    pltpu.make_async_remote_copy(
+                        src_ref=sums_reply.at[r, other], dst_ref=sums_remote.at[p, row],
+                        send_sem=srep_send.at[p], recv_sem=srep_recv.at[p],
+                        device_id=(other, pair * 2 + r), device_id_type=MESH,
+                    ).start()
+
+            each_peer(answer)
+            for j in range(1, pairs):
+                sums_forward(p, j).start()
 
     def relay(p, s, steps):
         for kind, q in [(text[0], int(text[1:] or 0)) for text in steps]:
@@ -320,6 +345,11 @@
             got = sums_remote.at[p, pl.ds(0, peers)]
             pltpu.make_async_copy(got, got, srep_recv.at[p]).wait()
 
+            @pl.when(low == 0)
+            def _():
+                for j in range(1, pairs):
+                    sums_forward(p, j).wait_recv()
+
             def fold_sums(other):
                 sums[p][group + other] = sums_remote[p, other]
 
@@ -348,10 +378,16 @@
             sent = reply.at[s, r, pl.ds(0, peers), pl.ds(0, block_rows // 2), :]
             pltpu.make_async_copy(sent, sent, rep_send.at[p, s]).wait()
         if s == STREAMS - 1:
-            for j in range(1, n_cols):
-                sums_to(p, j).wait_send()
-            sent = sums_reply.at[pl.ds(0, peers)]
-            pltpu.make_async_copy(sent, sent, srep_send.at[p]).wait()
+            for j in range(1, pairs):
+                sums_far(p, j, low).wait_send()
+            sums_near(p).wait_send()
+
+            @pl.when(low == 1)
+            def _():
+                sent = sums_reply.at[:, pl.ds(0, peers)]
+                pltpu.make_async_copy(sent, sent, srep_send.at[p]).wait()
+                for j in range(1, pairs):
+                    sums_forward(p, j).wait_send()
 
 
     for s in range(STREAMS):
@@ -410,7 +446,6 @@
     padded = -(-n_rows // LANES) * LANES
     pairs = max(n_cols // 2, 2)
     span = (pairs - 1) * 2 * blocks_dev
-    others = max(n_cols - 1, 1)
     unit = block_rows // sum(CHUNK_PARTS)
     dma = pltpu.SemaphoreType.DMA
     vmem = pl.BlockSpec(memory_space=pltpu.VMEM)
@@ -443,7 +478,7 @@
             ],
             [pltpu.VMEM((group + n_rows, 1, block_rows), jnp.float32) for _ in range(2)],
             pltpu.VMEM((2, n_rows, 1, block_rows), jnp.float32),
-            pltpu.VMEM((n_rows, 1, block_rows), jnp.float32),
+            pltpu.VMEM((2, n_rows, 1, block_rows), jnp.float32),
             pltpu.VMEM((blocks_dev, 1, block_rows), jnp.float32),
             pltpu.VMEM((nodes, lanes), jnp.float32),
             pltpu.VMEM((STREAMS, nodes, lanes), jnp.float32),
@@ -467,7 +502,7 @@
             dma((2, STREAMS, pairs - 1, CHUNKS, 2)), dma((2, STREAMS, pairs - 1, CHUNKS, 2)),
             dma((2, STREAMS, pairs - 1, CHUNKS)), dma((2, STREAMS, pairs - 1, CHUNKS)),
             dma((2, STREAMS)), dma((2, STREAMS, CHUNKS)),
-            dma((2, others)), dma((2, others)),
+            dma((2, 2 * pairs - 1)), dma((2, 3 * pairs - 2)),
             dma((2,)), dma((2,)),
         ],
         compiler_params=pltpu.CompilerParams(

time: 68.8 us -> 67.3 us (0.978)
  Pallas kernels: 66.6 us -> 65.1 us
    pallas_call x1, Pallas kernels: 66.6 us -> 65.1 us  [local(): pl.pallas_call(functools.partial(kernel, n_rows, n_cols, blocks_dev, degr...]
where the time goes in v4:
time: 67.3 us; the launch traced here: 67.2 us
  Pallas kernels  65.1 us (97%)
  local copies, waits for them, and re-layouts  2.06 us (3%)
    pallas_call x1, Pallas kernels, local(): pl.pallas_call(functools.partial(kernel, n_rows, n_cols, blocks_dev, degr...  65.1 us
    unnamed x1, local copies, waits for them, and re-layouts  2.06 us

profile of v4, /device:TPU:0, one launch (start us, length us, event | category | flops | bytes accessed | tf_op | source)
XLA Modules:
  0.0 67.2 jit_solution(11119034608215887545)
XLA Ops:
  0.0 65.1 %shard_map.55 = f32[768,256]{1,0:T(8,128)} custom-call(s32[6,12]{1,0:T(8,128)} %col_block_hbm.1, f32[768,256]{1,0:T(8,128)} %prior_hbm.1, s32[6,128]{1,0:T(8,128)} %bitcast.2, s32[6,128]{1,0:T(8,128)} %bitcast.3, bf16[6,12,128,128]{3,2,1,0:T(8,128)(2,1)} %adj_hbm.1), custom_call_target="tpu_custom_call" | custom-call | tf_op jit(solution)/shard_map/pallas_call | solution.py:452
  65.1 2.1 %copy.7 = f32[768,256]{1,0:T(8,128)} copy(f32[768,256]{1,0:T(8,128)} %shard_map.55) | data formatting | bytes 1572864

commit v5 on v4

--- a/solution.py
+++ b/solution.py
@@ -12,7 +12,7 @@
 CHUNK_PARTS = (2, 2, 4)
 EARLY = ("A0", "A1")
 LATE = ("A2",)
-BETWEEN = (("M0", "M1", "A0", "A1"), ("U", "M0", "A0", "M1", "A1"))
+BETWEEN = (("M0", "M1", "A0", "A1"), ("U", "A0", "M0", "A1", "M1"))
 CHUNKS = len(CHUNK_PARTS)
 HEAD = [f"G{q}" for q in range(CHUNKS)]
 ALPHA = 0.85

time: 67.3 us -> 68.4 us (1.016)
  Pallas kernels: 65.1 us -> 66.2 us
    pallas_call x1, Pallas kernels: 65.1 us -> 66.2 us  [local(): pl.pallas_call(functools.partial(kernel, n_rows, n_cols, blocks_dev, degr...]
where the time goes in v5:
time: 68.4 us; the launch traced here: 68.3 us
  Pallas kernels  66.2 us (97%)
  local copies, waits for them, and re-layouts  2.06 us (3%)
    pallas_call x1, Pallas kernels, local(): pl.pallas_call(functools.partial(kernel, n_rows, n_cols, blocks_dev, degr...  66.2 us
    unnamed x1, local copies, waits for them, and re-layouts  2.06 us

profile of v5, /device:TPU:0, one launch (start us, length us, event | category | flops | bytes accessed | tf_op | source)
XLA Modules:
  0.0 68.3 jit_solution(3091222752438439081)
XLA Ops:
  0.0 66.2 %shard_map.55 = f32[768,256]{1,0:T(8,128)} custom-call(s32[6,12]{1,0:T(8,128)} %col_block_hbm.1, f32[768,256]{1,0:T(8,128)} %prior_hbm.1, s32[6,128]{1,0:T(8,128)} %bitcast.2, s32[6,128]{1,0:T(8,128)} %bitcast.3, bf16[6,12,128,128]{3,2,1,0:T(8,128)(2,1)} %adj_hbm.1), custom_call_target="tpu_custom_call" | custom-call | tf_op jit(solution)/shard_map/pallas_call | solution.py:452
  66.2 2.1 %copy.7 = f32[768,256]{1,0:T(8,128)} copy(f32[768,256]{1,0:T(8,128)} %shard_map.55) | data formatting | bytes 1572864
